TPU v7x, 128 devices: a whole 4x4x4 slice. The times are simulated.
128 devices in a mesh: dev: 128 (over z, x, y, core).
Axes of the slice: x: 4, y: 4, z: 4, core: 2. Of those that a mesh axis runs over, the one named last changes fastest.
Arguments:
- state: float32 [2, 4194304], P(None, 'dev'), as said below
- angles: float32 [22, 3], replicated, may hold values from -3.140625 to 3.140625
- sample_high: int32 [1048576, 1], P('dev'), may hold values from 0 to 127; in each aligned block of 8192 rows (0 to 8191, 8192 to 16383, ...) at most 256 rows name the same one
- sample_low: int32 [1048576], P('dev'), may hold values from 0 to 32767
- marginal_qubits: int32 [10], replicated, may hold values from 0 to 21, as said below
Outputs:
- sample_probs: float32 [1048576], P('dev')
- histogram: float32 [1024], P('dev')
- fidelity: float32 [], replicated
Inputs may be any that keep to these rules, and one draw needn't show every extreme that they name: The state is unit noise times a product over qubits of factors between exp(-0.2) and exp(0.2). `marginal_qubits`: 10 different qubit numbers. `sample_high`: among the rows of one device no value occurs more than 256 times, and in some devices one value occurs exactly 256 times.
All inputs are finite; a program needn't handle non-finite values.
Results may differ from a plain program's by a relative error of at most 0.00075.
Values sent between devices are 32-bit elements.
A program may use at most 64 MiB of HBM per device.

v0:
```python
import functools

import jax
import jax.numpy as jnp
from jax import lax
from jax.experimental import pallas as pl
from jax.experimental.pallas import tpu as pltpu
from jax.sharding import PartitionSpec as P

LANES = 128
SUBLANES = 8
f32 = jnp.float32
bf16 = jnp.bfloat16
i32 = jnp.int32


def iota(shape, dim):
    return lax.broadcasted_iota(i32, shape, dim)


def gate_rows(angles, qubits):
    sub = iota((SUBLANES, LANES), 0)

    def column(j):
        blocks = []
        for first in range(0, qubits, SUBLANES):
            block = jnp.zeros((SUBLANES, LANES), f32)
            for q in range(first, min(first + SUBLANES, qubits)):
                block = jnp.where(sub == q - first, angles[j, q], block)
            blocks.append(block)
        return jnp.concatenate(blocks, axis=0)

    theta, first, second = column(0), column(1), column(2)
    cosine, sine = jnp.cos(theta), jnp.sin(theta)
    joint = first + second
    return [
        cosine,
        jnp.zeros_like(cosine),
        -jnp.cos(second) * sine,
        -jnp.sin(second) * sine,
        jnp.cos(first) * sine,
        jnp.sin(first) * sine,
        jnp.cos(joint) * cosine,
        jnp.sin(joint) * cosine,
    ]


def leading_gate(xr, xi, bit, u):
    n, s, lanes = xr.shape
    shape = (n >> (bit + 1), 2, 1 << bit, s, lanes)
    xr, xi = xr.reshape(shape), xi.reshape(shape)
    ar, ai, br, bi = xr[:, 0], xi[:, 0], xr[:, 1], xi[:, 1]
    outs_r, outs_i = [], []
    for row in range(2):
        pr, pi, qr, qi = u[4 * row : 4 * row + 4]
        outs_r.append(pr * ar - pi * ai + (qr * br - qi * bi))
        outs_i.append(pr * ai + pi * ar + (qr * bi + qi * br))
    return (
        jnp.stack(outs_r, 1).reshape(n, s, lanes),
        jnp.stack(outs_i, 1).reshape(n, s, lanes),
    )


def sublane_gate(xr, xi, bit, u):
    step = 1 << bit
    high = ((iota((SUBLANES, LANES), 0) >> bit) & 1) == 1

    def swap(x):
        down = pltpu.roll(x, step, 1)
        if 2 * step == SUBLANES:
            return down
        return jnp.where(high[None], down, pltpu.roll(x, SUBLANES - step, 1))

    keep_r = jnp.where(high, u[6], u[0])[None]
    keep_i = jnp.where(high, u[7], u[1])[None]
    cross_r = jnp.where(high, u[4], u[2])[None]
    cross_i = jnp.where(high, u[5], u[3])[None]
    yr, yi = swap(xr), swap(xi)
    return (
        keep_r * xr - keep_i * xi + (cross_r * yr - cross_i * yi),
        keep_r * xi + keep_i * xr + (cross_r * yi + cross_i * yr),
    )


def lane_matrix(units):
    shape = (LANES, LANES)
    row, col = iota(shape, 0), iota(shape, 1)
    mr = mi = None
    for bit, u in enumerate(units):
        rb, cb = ((row >> bit) & 1) == 1, ((col >> bit) & 1) == 1
        gr = jnp.where(cb, jnp.where(rb, u[6], u[4]), jnp.where(rb, u[2], u[0]))
        gi = jnp.where(cb, jnp.where(rb, u[7], u[5]), jnp.where(rb, u[3], u[1]))
        if mr is None:
            mr, mi = gr, gi
        else:
            mr, mi = mr * gr - mi * gi, mr * gi + mi * gr
    return mr, mi


def cut(x, depth):
    rows = x.shape[0]
    x = x.reshape(rows // SUBLANES, SUBLANES, LANES)
    per = SUBLANES // depth
    if per == 1:
        return x
    parts = [x[:, k * depth : (k + 1) * depth] for k in range(per)]
    return jnp.stack(parts, 1).reshape(rows // depth, depth, LANES)


def join(x):
    n, depth, _ = x.shape
    per = SUBLANES // depth
    if per > 1:
        x = x.reshape(n // per, per, depth, LANES)
        x = jnp.concatenate([x[:, k] for k in range(per)], axis=1)
    return x.reshape(n * depth, LANES)


def halves(x):
    top = x.astype(bf16)
    return top, (x - top.astype(f32)).astype(bf16)


def one_hot(row, count):
    wide = jnp.broadcast_to(row.astype(f32), (16, LANES)).astype(bf16)
    ids = iota((count, LANES), 0).astype(f32).astype(bf16).reshape(count // 16, 16, LANES)
    hot = jnp.where(ids == wide[None], jnp.ones((), bf16), jnp.zeros((), bf16))
    return hot.reshape(count, LANES)


def split_table(table):
    flipped = table.T
    top, rest = halves(flipped)
    return jnp.concatenate([top, rest], axis=0)


def lookup_dot(table, upper, lower):
    rows = upper.shape[0]
    count = table.shape[1]
    hot = jnp.concatenate([one_hot(upper[r : r + 1], count) for r in range(rows)], axis=1)
    both = jnp.dot(table, hot, preferred_element_type=f32)
    lane_ids = iota((LANES, LANES), 0)
    found = []
    for r in range(rows):
        part = slice(r * LANES, (r + 1) * LANES)
        value = both[:LANES, part] + both[LANES:, part]
        value = jnp.where(lane_ids == lower[r : r + 1], value, 0.0)
        found.append(jnp.sum(value, axis=0, keepdims=True))
    return jnp.concatenate(found, axis=0)


def lookup_lanes(table_ref, upper, lower):
    rows = upper.shape[0]
    if rows < SUBLANES:
        upper = jnp.concatenate([upper] * (SUBLANES // rows), axis=0)
        lower = jnp.concatenate([lower] * (SUBLANES // rows), axis=0)
    shape = (SUBLANES, LANES)
    bits = table_ref.shape[0].bit_length() - 1
    high = [((upper >> bit) & 1) == 1 for bit in range(bits)]

    def pick(first, bit):
        if bit < 0:
            line = jnp.broadcast_to(table_ref[first : first + 1], shape)
            return jnp.take_along_axis(line, lower, axis=1, mode="promise_in_bounds")
        zero = pick(first, bit - 1)
        return jnp.where(high[bit], pick(first + (1 << bit), bit - 1), zero)

    return pick(0, bits - 1)[:rows]


def lookup_both(table, plain, wanted, other):
    one = lookup_dot(table, wanted[0], wanted[1])
    return one, lookup_lanes(plain, other[0], other[1])


def kernel(
    sizes,
    angles,
    marg,
    state,
    owner_ref,
    low_ref,
    probs_ref,
    hist_ref,
    fid_ref,
    amp_out,
    amp_in,
    wt_out,
    wt_in,
    req_out,
    req_in,
    ans_out,
    ans_in,
    his_out,
    his_in,
    tot_out,
    tot_in,
    code_ref,
    rank_ref,
    table_ref,
    plain_ref,
    back_ref,
    gates,
    sends,
    recvs,
    req_recvs,
):
    devices, depth, capacity_rows, marg_count = sizes
    me = lax.axis_index("dev")
    global_bits = devices.bit_length() - 1
    rows = state.shape[0] // 2
    row_bits = rows.bit_length() - 1
    local_bits = row_bits + 7
    codes = devices * capacity_rows

    def peer(k):
        return lax.rem(me + k, devices)

    def copy(channel, src, dst, target):
        return pltpu.make_async_remote_copy(
            src_ref=src,
            dst_ref=dst,
            send_sem=sends.at[channel],
            recv_sem=recvs.at[channel],
            device_id=(target,),
            device_id_type=pl.DeviceIdType.MESH,
        )

    def scatter(channel, out, into):
        @pl.loop(1, devices)
        def _(k):
            target = peer(k)
            copy(channel, out.at[target], into.at[me], target).start()

        into[me] = out[me]

    def spread(channel, out, into):
        @pl.loop(1, devices)
        def _(k):
            copy(channel, out.at[0], into.at[me], peer(k)).start()

        into[me] = out[0]

    def all_of(channel, into):
        many = into.at[pl.ds(0, devices - 1)]
        return copy(channel, many, many, peer(1))

    def ask(src, source, target):
        return pltpu.make_async_remote_copy(
            src_ref=src,
            dst_ref=req_in.at[source],
            send_sem=sends.at[1],
            recv_sem=req_recvs.at[source],
            device_id=(target,),
            device_id_type=pl.DeviceIdType.MESH,
        )

    barrier = pltpu.get_barrier_semaphore()

    @pl.loop(1, devices)
    def _(k):
        pl.semaphore_signal(
            barrier, inc=1, device_id=(peer(k),), device_id_type=pl.DeviceIdType.MESH
        )

    for e, entry in enumerate(gate_rows(angles, global_bits + local_bits)):
        gates[e] = entry

    def unit(qubit):
        return [gates[e, qubit : qubit + 1] for e in range(8)]

    mr, mi = lane_matrix([unit(q) for q in range(7)])
    mixed = jnp.concatenate(
        [jnp.concatenate([mr, mi], axis=1), jnp.concatenate([-mi, mr], axis=1)], axis=0
    )
    both = jnp.concatenate(
        [state[pl.ds(0, rows, stride=2)], state[pl.ds(1, rows, stride=2)]], axis=1
    )
    both = jnp.dot(both, mixed, precision=lax.Precision.HIGHEST, preferred_element_type=f32)
    xr = both[:, :LANES].reshape(rows // SUBLANES, SUBLANES, LANES)
    xi = both[:, LANES:].reshape(rows // SUBLANES, SUBLANES, LANES)
    for bit in range(3):
        xr, xi = sublane_gate(xr, xi, bit, unit(7 + bit))
    for bit in range(row_bits - 3):
        xr, xi = leading_gate(xr, xi, bit, unit(10 + bit))
    amp_out[:, 0] = cut(xr.reshape(rows, LANES), depth)
    amp_out[:, 1] = cut(xi.reshape(rows, LANES), depth)

    pl.semaphore_wait(barrier, devices - 1)
    scatter(0, amp_out, amp_in)

    samp_rows = owner_ref.shape[0]
    owner = owner_ref[...]
    owner_ids = iota((devices, LANES), 0)
    chunks = samp_rows // 2
    hot_rows = [(owner_ids == owner[r : r + 1]) for r in range(samp_rows)]
    pieces = [h.astype(f32).astype(bf16) for h in hot_rows]
    stacked = jnp.concatenate(
        [jnp.concatenate(pieces[2 * c : 2 * c + 2], axis=1) for c in range(chunks)], axis=0
    )
    tri_shape = (2 * LANES, 3 * LANES)
    tri_row, tri_col = iota(tri_shape, 0), iota(tri_shape, 1)
    tri = ((tri_row < tri_col) | (tri_col >= 2 * LANES)).astype(f32).astype(bf16)
    counts = jnp.dot(stacked, tri, preferred_element_type=f32)
    before = jnp.zeros((devices, LANES), f32)
    ranks = []
    for c in range(chunks):
        block = counts[c * devices : (c + 1) * devices]
        for h in range(2):
            spot = block[:, h * LANES : (h + 1) * LANES] + before
            mine = owner_ids == owner[2 * c + h : 2 * c + h + 1]
            ranks.append(jnp.sum(jnp.where(mine, spot, 0.0), axis=0, keepdims=True))
        before = before + block[:, 2 * LANES :]
    ranking = jnp.concatenate(ranks, axis=0).astype(i32)
    code_ref[...] = owner * capacity_rows + (ranking >> 7)
    rank_ref[...] = ranking & (LANES - 1)

    lane_ids = iota((LANES, LANES), 0)
    steps = samp_rows // SUBLANES

    def place(t, placed):
        window = pl.ds(pl.multiple_of(t * SUBLANES, SUBLANES), SUBLANES)
        code, rank, low = code_ref[window], rank_ref[window], low_ref[window] + 1
        low_top = (low >> 8).astype(f32)
        low_rest = (low & 255).astype(f32)
        hot = jnp.concatenate([one_hot(code[r : r + 1], codes) for r in range(SUBLANES)], axis=1)
        tops, rests = [], []
        for r in range(SUBLANES):
            here = lane_ids == rank[r : r + 1]
            tops.append(jnp.where(here, low_top[r : r + 1], 0.0).astype(bf16))
            rests.append(jnp.where(here, low_rest[r : r + 1], 0.0).astype(bf16))
        values = jnp.concatenate(
            [jnp.concatenate(tops, axis=1), jnp.concatenate(rests, axis=1)], axis=0
        )
        return placed + lax.dot_general(
            hot, values, (((1,), (1,)), ((), ())), preferred_element_type=f32
        )

    placed = lax.fori_loop(0, steps, place, jnp.zeros((codes, 2 * LANES), f32))
    wanted = (placed[:, :LANES] * 256.0 + placed[:, LANES:]).astype(i32) - 1
    req_out[...] = cut(wanted, capacity_rows)

    all_of(0, amp_in).wait_recv()
    xr, xi = amp_in[:, 0], amp_in[:, 1]
    for bit in range(global_bits):
        xr, xi = leading_gate(xr, xi, bit, unit(local_bits + bit))
    weight = xr * xr + xi * xi
    wt_out[...] = weight
    scatter(2, wt_out, wt_in)

    @pl.loop(1, devices)
    def _(k):
        target = peer(k)
        ask(req_out.at[target], me, target).start()

    weight = join(weight)
    norm_part = jnp.sum(weight, axis=0, keepdims=True)
    low_depth = depth.bit_length() - 1
    code_shape = (rows, LANES)
    row_id = iota(code_shape, 0)
    row_value = (
        ((row_id >> low_depth) << local_bits)
        + (me << (7 + low_depth))
        + ((row_id & (depth - 1)) << 7)
    )
    lane_value = iota((LANES, LANES), 0)
    row_code = jnp.zeros(code_shape, i32)
    lane_code = jnp.zeros((LANES, LANES), i32)
    lane_mask = jnp.zeros((), i32)
    for k in range(marg_count):
        qubit = marg[0, k]
        row_code = row_code + (((row_value >> qubit) & 1) << k)
        lane_code = lane_code + (((lane_value >> qubit) & 1) << k)
        lane_mask = lane_mask + jnp.where(qubit < 7, 1 << k, 0)
    bins = 2**marg_count
    top, rest = halves(weight)
    split = jnp.concatenate([top, rest], axis=0)
    @pl.loop(0, bins // LANES)
    def _(c):
        bin_id = c * LANES + iota((1, LANES), 1)
        lane_part = bin_id & lane_mask
        lane_hot = (lane_code == lane_part).astype(f32).astype(bf16)
        folded = jnp.dot(split, lane_hot, preferred_element_type=f32)
        folded = folded[:rows] + folded[rows:]
        picked = jnp.where(row_code == bin_id - lane_part, folded, 0.0)
        his_out[0, pl.ds(c, 1)] = jnp.sum(picked, axis=0, keepdims=True)


    all_of(2, wt_in).wait_recv()
    spread(4, his_out, his_in)
    plain_ref[...] = join(wt_in[...])
    table_ref[...] = split_table(plain_ref[...])

    def parts(wanted):
        return wanted >> 7, wanted & (LANES - 1)

    def answers(wanted, other):
        found, second = lookup_both(
            table_ref[:, 0:rows], plain_ref, parts(wanted), parts(other)
        )
        return found, jnp.where(other >= 0, second, 0.0)

    def asked(k):
        source = peer(devices - k)
        ask(req_out.at[source], source, source).wait_recv()
        return source

    def send(source, found):
        ans_out[source] = found
        copy(3, ans_out.at[source], ans_in.at[me], source).start()

    source = asked(1)
    found, own = answers(req_in[source], req_out[me])
    send(source, found)
    ans_in[me] = own

    def reply(t, total):
        first, second = asked(2 * t), asked(2 * t + 1)
        found, other = answers(req_in[first], req_in[second])
        send(first, found)
        send(second, other)
        return total + jnp.sum(found + other, axis=0, keepdims=True)

    total = jnp.sum(found + own, axis=0, keepdims=True)
    total = lax.fori_loop(1, devices // 2, reply, total)
    tot_out[0, 0:1] = total
    tot_out[0, 1:2] = norm_part
    spread(5, tot_out, tot_in)

    all_of(3, ans_in).wait_recv()
    back_ref[...] = join(ans_in[...])
    table_ref[:, 0:codes] = split_table(back_ref[...])

    def fetch(t, carry):
        one = pl.ds(pl.multiple_of(2 * t * SUBLANES, SUBLANES), SUBLANES)
        two = pl.ds(pl.multiple_of((2 * t + 1) * SUBLANES, SUBLANES), SUBLANES)
        probs_ref[one], probs_ref[two] = lookup_both(
            table_ref[:, 0:codes],
            back_ref,
            (code_ref[one], rank_ref[one]),
            (code_ref[two], rank_ref[two]),
        )
        return carry

    lax.fori_loop(0, steps // 2, fetch, 0)
    all_of(5, tot_in).wait_recv()
    all_of(4, his_in).wait_recv()
    hist_ref[...] = jnp.sum(his_in[...], axis=0)
    fid_ref[...] = jnp.sum(tot_in[...], axis=0)

    for channel, into in enumerate((amp_in, req_in, wt_in, ans_in, his_in, tot_in)):
        all_of(channel, into).wait_send()


def finish(sizes, values, hist, totals, probs_ref, mine_ref, fid_ref):
    amps_total, samples = sizes
    bins, mine = float(hist.shape[0] * LANES), mine_ref.shape[1]
    start = lax.axis_index("dev") * mine
    sums = jnp.sum(totals[...], axis=1, keepdims=True)
    total, norm = sums[0:1], sums[1:2]
    probs_ref[...] = amps_total * (values[...] / norm)
    line = hist[pl.ds(start // LANES, 1)]
    line = jnp.broadcast_to(line, (SUBLANES, LANES))
    line = pltpu.roll(line, (LANES - start % LANES) % LANES, 1)
    mine_ref[...] = bins * (line[0:1, :mine] / norm)
    fid_ref[...] = amps_total * (total / norm) / samples - 1.0


def shards(state, angles, sample_high, sample_low, marginal_qubits):
    devices = lax.axis_size("dev")
    amps_local = state.shape[1]
    samp_local = sample_low.shape[0]
    marg_count = marginal_qubits.shape[0]
    bins = 2**marg_count
    depth = amps_local // devices // LANES
    capacity_rows = 4 * samp_local // devices // LANES
    rows = amps_local // LANES
    samp_rows = samp_local // LANES
    sizes = (
        devices,
        depth,
        capacity_rows,
        marg_count,
    )
    vmem = pl.BlockSpec(memory_space=pltpu.VMEM)
    smem = pl.BlockSpec(memory_space=pltpu.SMEM)
    codes = devices * capacity_rows
    bin_rows = bins // LANES
    values, hist, totals = pl.pallas_call(
        functools.partial(kernel, sizes),
        out_shape=(
            jax.ShapeDtypeStruct((samp_rows, LANES), f32),
            jax.ShapeDtypeStruct((bin_rows, LANES), f32),
            jax.ShapeDtypeStruct((2, LANES), f32),
        ),
        in_specs=[smem, smem, vmem, vmem, vmem],
        out_specs=(vmem, vmem, vmem),
        scratch_shapes=[
            pltpu.VMEM((devices, 2, depth, LANES), f32),
            pltpu.VMEM((devices, 2, depth, LANES), f32),
            pltpu.VMEM((devices, depth, LANES), f32),
            pltpu.VMEM((devices, depth, LANES), f32),
            pltpu.VMEM((devices, capacity_rows, LANES), i32),
            pltpu.VMEM((devices, capacity_rows, LANES), i32),
            pltpu.VMEM((devices, capacity_rows, LANES), f32),
            pltpu.VMEM((devices, capacity_rows, LANES), f32),
            pltpu.VMEM((1, bin_rows, LANES), f32),
            pltpu.VMEM((devices, bin_rows, LANES), f32),
            pltpu.VMEM((1, 2, LANES), f32),
            pltpu.VMEM((devices, 2, LANES), f32),
            pltpu.VMEM((samp_rows, LANES), i32),
            pltpu.VMEM((samp_rows, LANES), i32),
            pltpu.VMEM((2 * LANES, max(rows, codes)), bf16),
            pltpu.VMEM((rows, LANES), f32),
            pltpu.VMEM((codes, LANES), f32),
            pltpu.VMEM((8, -(-angles.shape[0] // SUBLANES) * SUBLANES, LANES), f32),
            pltpu.SemaphoreType.DMA((6,)),
            pltpu.SemaphoreType.DMA((6,)),
            pltpu.SemaphoreType.DMA((devices,)),
        ],
        compiler_params=pltpu.CompilerParams(collective_id=0, has_side_effects=True),
        name="circuit",
    )(
        angles.T,
        marginal_qubits.reshape(1, marg_count),
        state.reshape(2, rows, LANES).transpose(1, 0, 2).reshape(2 * rows, LANES),
        sample_high.reshape(samp_rows, LANES),
        sample_low.reshape(samp_rows, LANES),
    )
    probs, mine, fid = pl.pallas_call(
        functools.partial(finish, (float(amps_local * devices), float(samp_local * devices))),
        out_shape=(
            jax.ShapeDtypeStruct((samp_rows, LANES), f32),
            jax.ShapeDtypeStruct((1, bins // devices), f32),
            jax.ShapeDtypeStruct((1, 1), f32),
        ),
        in_specs=[vmem, vmem, vmem],
        out_specs=(vmem, vmem, vmem),
        name="finish",
    )(values, hist, totals)
    return probs.reshape(samp_local), mine.reshape(bins // devices), fid.reshape(())


def solution(mesh):
    return jax.shard_map(
        shards,
        mesh=mesh,
        in_specs=(P(None, "dev"), P(), P("dev", None), P("dev"), P()),
        out_specs=(P("dev"), P("dev"), P()),
        check_vma=False,
    )
```

profile of v0, /device:TPU:1, one launch (start us, length us, event | category | flops | bytes accessed | tf_op | source)
XLA Modules:
  0.0 65.0 jit_solution(18133825816166610843)
XLA Ops:
  0.6 62.9 %circuit.1 = (f32[64,128]{1,0:T(8,128)}, f32[8,128]{1,0:T(8,128)}, f32[2,128]{1,0:T(2,128)}) custom-call(f32[3,22]{1,0:T(4,128)} %bitcast.15, s32[1,10]{1,0:T(1,128)} %bitcast.16, f32[512,128]{1,0:T(8,128)} %bitcast.12, s32[64,128]{1,0:T(8,128)} %bitcast.13, s32[64,128]{1,0:T(8,128)} %bitcast.14), custom_call_target="tpu_custom_call" | custom-call | tf_op jit(solution)/shard_map/circuit/pallas_call | solution.py:489
  63.5 1.5 %finish.1 = (f32[64,128]{1,0:T(8,128)}, f32[1,8]{1,0:T(1,128)}, f32[1,1]{1,0:T(1,128)}) custom-call(f32[64,128]{1,0:T(8,128)} %get-tuple-element.9.values, f32[8,128]{1,0:T(8,128)} %get-tuple-element.10.hist, f32[2,128]{1,0:T(2,128)} %get-tuple-element.11.totals), custom_call_target="tpu_custom_call" | custom-call | tf_op jit(solution)/shard_map/finish/pallas_call | solution.py:530
where the time goes:
time: 65.2 us; the launch traced here: 65 us
  Pallas kernels  64.3 us (99%)
    pallas_call x1, Pallas kernels, shards(): pl.pallas_call(functools.partial(kernel, sizes), out_shape=(jax.ShapeDtyp...  62.9 us
    pallas_call x1, Pallas kernels, shards(): pl.pallas_call(functools.partial(finish, (float(amps_local * devices), fl...  1.47 us

commit v1 on v0

--- a/solution.py
+++ b/solution.py
@@ -97,6 +97,21 @@
     return mr, mi
 
 
+def row_matrix(units):
+    shape = (LANES, LANES)
+    row, col = iota(shape, 0), iota(shape, 1)
+    mr = mi = None
+    for bit, u in enumerate(units):
+        rb, cb = ((row >> bit) & 1) == 1, ((col >> bit) & 1) == 1
+        gr = jnp.where(rb, jnp.where(cb, u[6], u[4]), jnp.where(cb, u[2], u[0]))
+        gi = jnp.where(rb, jnp.where(cb, u[7], u[5]), jnp.where(cb, u[3], u[1]))
+        if mr is None:
+            mr, mi = gr, gi
+        else:
+            mr, mi = mr * gr - mi * gi, mr * gi + mi * gr
+    return mr, mi
+
+
 def cut(x, depth):
     rows = x.shape[0]
     x = x.reshape(rows // SUBLANES, SUBLANES, LANES)
@@ -134,43 +149,23 @@
     return jnp.concatenate([top, rest], axis=0)
 
 
-def lookup_dot(table, upper, lower):
+def lookup(table, upper, lower):
     rows = upper.shape[0]
     count = table.shape[1]
     hot = jnp.concatenate([one_hot(upper[r : r + 1], count) for r in range(rows)], axis=1)
     both = jnp.dot(table, hot, preferred_element_type=f32)
-    lane_ids = iota((LANES, LANES), 0)
+    sub = iota((SUBLANES, LANES), 0)
     found = []
     for r in range(rows):
         part = slice(r * LANES, (r + 1) * LANES)
-        value = both[:LANES, part] + both[LANES:, part]
-        value = jnp.where(lane_ids == lower[r : r + 1], value, 0.0)
+        value = (both[:LANES, part] + both[LANES:, part]).reshape(LANES // SUBLANES, SUBLANES, LANES)
+        low = jnp.broadcast_to(lower[r : r + 1], (SUBLANES, LANES))
+        for bit in (6, 5, 4, 3):
+            half = value.shape[0] // 2
+            value = jnp.where((((low >> bit) & 1) == 1)[None], value[half:], value[:half])
+        value = jnp.where(sub == (low & (SUBLANES - 1)), value[0], 0.0)
         found.append(jnp.sum(value, axis=0, keepdims=True))
     return jnp.concatenate(found, axis=0)
-
-
-def lookup_lanes(table_ref, upper, lower):
-    rows = upper.shape[0]
-    if rows < SUBLANES:
-        upper = jnp.concatenate([upper] * (SUBLANES // rows), axis=0)
-        lower = jnp.concatenate([lower] * (SUBLANES // rows), axis=0)
-    shape = (SUBLANES, LANES)
-    bits = table_ref.shape[0].bit_length() - 1
-    high = [((upper >> bit) & 1) == 1 for bit in range(bits)]
-
-    def pick(first, bit):
-        if bit < 0:
-            line = jnp.broadcast_to(table_ref[first : first + 1], shape)
-            return jnp.take_along_axis(line, lower, axis=1, mode="promise_in_bounds")
-        zero = pick(first, bit - 1)
-        return jnp.where(high[bit], pick(first + (1 << bit), bit - 1), zero)
-
-    return pick(0, bits - 1)[:rows]
-
-
-def lookup_both(table, plain, wanted, other):
-    one = lookup_dot(table, wanted[0], wanted[1])
-    return one, lookup_lanes(plain, other[0], other[1])
 
 
 def kernel(
@@ -187,8 +182,6 @@
     amp_in,
     wt_out,
     wt_in,
-    req_out,
-    req_in,
     ans_out,
     ans_in,
     his_out,
@@ -197,13 +190,12 @@
     tot_in,
     code_ref,
     rank_ref,
+    req_ref,
     table_ref,
-    plain_ref,
-    back_ref,
+    global_ref,
     gates,
     sends,
     recvs,
-    req_recvs,
 ):
     devices, depth, capacity_rows, marg_count = sizes
     me = lax.axis_index("dev")
@@ -245,16 +237,6 @@
         many = into.at[pl.ds(0, devices - 1)]
         return copy(channel, many, many, peer(1))
 
-    def ask(src, source, target):
-        return pltpu.make_async_remote_copy(
-            src_ref=src,
-            dst_ref=req_in.at[source],
-            send_sem=sends.at[1],
-            recv_sem=req_recvs.at[source],
-            device_id=(target,),
-            device_id_type=pl.DeviceIdType.MESH,
-        )
-
     barrier = pltpu.get_barrier_semaphore()
 
     @pl.loop(1, devices)
@@ -286,6 +268,11 @@
     amp_out[:, 0] = cut(xr.reshape(rows, LANES), depth)
     amp_out[:, 1] = cut(xi.reshape(rows, LANES), depth)
 
+    mr, mi = row_matrix([unit(local_bits + q) for q in range(global_bits)])
+    mixed = jnp.concatenate(
+        [jnp.concatenate([mr, -mi], axis=1), jnp.concatenate([mi, mr], axis=1)], axis=0
+    )
+    global_ref[0], global_ref[1] = halves(mixed)
     pl.semaphore_wait(barrier, devices - 1)
     scatter(0, amp_out, amp_in)
 
@@ -337,31 +324,38 @@
         )
 
     placed = lax.fori_loop(0, steps, place, jnp.zeros((codes, 2 * LANES), f32))
-    wanted = (placed[:, :LANES] * 256.0 + placed[:, LANES:]).astype(i32) - 1
-    req_out[...] = cut(wanted, capacity_rows)
+    wanted = placed[:, :LANES] * 256.0 + placed[:, LANES:] - 1.0
+    wt_out[:, depth:] = cut(wanted, capacity_rows)
 
     all_of(0, amp_in).wait_recv()
-    xr, xi = amp_in[:, 0], amp_in[:, 1]
-    for bit in range(global_bits):
-        xr, xi = leading_gate(xr, xi, bit, unit(local_bits + bit))
+    both = jnp.concatenate(
+        [
+            jnp.concatenate([amp_in[:, part, d] for d in range(depth)], axis=1)
+            for part in range(2)
+        ],
+        axis=0,
+    )
+    top, rest = halves(both)
+    both = jnp.dot(global_ref[0], top, preferred_element_type=f32) + (
+        jnp.dot(global_ref[0], rest, preferred_element_type=f32)
+        + jnp.dot(global_ref[1], top, preferred_element_type=f32)
+    )
+    xr, xi = both[:devices], both[devices:]
     weight = xr * xr + xi * xi
-    wt_out[...] = weight
-    scatter(2, wt_out, wt_in)
-
-    @pl.loop(1, devices)
-    def _(k):
-        target = peer(k)
-        ask(req_out.at[target], me, target).start()
-
-    weight = join(weight)
+    weights = [weight[:, d * LANES : (d + 1) * LANES] for d in range(depth)]
+    for d in range(depth):
+        wt_out[:, d] = weights[d]
+    scatter(1, wt_out, wt_in)
+
+    weight = jnp.concatenate(weights, axis=0)
     norm_part = jnp.sum(weight, axis=0, keepdims=True)
-    low_depth = depth.bit_length() - 1
+    owner_bits = devices.bit_length() - 1
     code_shape = (rows, LANES)
     row_id = iota(code_shape, 0)
     row_value = (
-        ((row_id >> low_depth) << local_bits)
-        + (me << (7 + low_depth))
-        + ((row_id & (depth - 1)) << 7)
+        ((row_id & (devices - 1)) << local_bits)
+        + me * (depth * LANES)
+        + ((row_id >> owner_bits) << 7)
     )
     lane_value = iota((LANES, LANES), 0)
     row_code = jnp.zeros(code_shape, i32)
@@ -383,84 +377,73 @@
         folded = jnp.dot(split, lane_hot, preferred_element_type=f32)
         folded = folded[:rows] + folded[rows:]
         picked = jnp.where(row_code == bin_id - lane_part, folded, 0.0)
-        his_out[0, pl.ds(c, 1)] = jnp.sum(picked, axis=0, keepdims=True)
-
-
-    all_of(2, wt_in).wait_recv()
-    spread(4, his_out, his_in)
-    plain_ref[...] = join(wt_in[...])
-    table_ref[...] = split_table(plain_ref[...])
-
-    def parts(wanted):
-        return wanted >> 7, wanted & (LANES - 1)
-
-    def answers(wanted, other):
-        found, second = lookup_both(
-            table_ref[:, 0:rows], plain_ref, parts(wanted), parts(other)
-        )
-        return found, jnp.where(other >= 0, second, 0.0)
-
-    def asked(k):
-        source = peer(devices - k)
-        ask(req_out.at[source], source, source).wait_recv()
-        return source
-
-    def send(source, found):
-        ans_out[source] = found
-        copy(3, ans_out.at[source], ans_in.at[me], source).start()
-
-    source = asked(1)
-    found, own = answers(req_in[source], req_out[me])
-    send(source, found)
-    ans_in[me] = own
-
-    def reply(t, total):
-        first, second = asked(2 * t), asked(2 * t + 1)
-        found, other = answers(req_in[first], req_in[second])
-        send(first, found)
-        send(second, other)
-        return total + jnp.sum(found + other, axis=0, keepdims=True)
-
-    total = jnp.sum(found + own, axis=0, keepdims=True)
-    total = lax.fori_loop(1, devices // 2, reply, total)
-    tot_out[0, 0:1] = total
-    tot_out[0, 1:2] = norm_part
-    spread(5, tot_out, tot_in)
-
-    all_of(3, ans_in).wait_recv()
-    back_ref[...] = join(ans_in[...])
-    table_ref[:, 0:codes] = split_table(back_ref[...])
-
-    def fetch(t, carry):
-        one = pl.ds(pl.multiple_of(2 * t * SUBLANES, SUBLANES), SUBLANES)
-        two = pl.ds(pl.multiple_of((2 * t + 1) * SUBLANES, SUBLANES), SUBLANES)
-        probs_ref[one], probs_ref[two] = lookup_both(
-            table_ref[:, 0:codes],
-            back_ref,
-            (code_ref[one], rank_ref[one]),
-            (code_ref[two], rank_ref[two]),
-        )
-        return carry
-
-    lax.fori_loop(0, steps // 2, fetch, 0)
-    all_of(5, tot_in).wait_recv()
-    all_of(4, his_in).wait_recv()
+        his_out[c, 0:1] = jnp.sum(picked, axis=0, keepdims=True)
+    for c in range(bins // LANES):
+        his_out[c, 1:2] = norm_part
+
+    bin_share = devices * LANES // bins
+
+    @pl.loop(1, devices)
+    def _(k):
+        target = peer(k)
+        copy(3, his_out.at[target // bin_share], his_in.at[me], target).start()
+
+    his_in[me] = his_out[me // bin_share]
+
+    all_of(1, wt_in).wait_recv()
+    table_ref[:, 0:rows] = split_table(join(wt_in[:, 0:depth]))
+    req_ref[...] = join(wt_in[:, depth:]).astype(i32)
+    group = 32 // capacity_rows
+    groups = devices // group
+    mine, spot = me // group, me % group
+
+    def answer(turn):
+        first = lax.rem(mine + turn, groups) * group
+        window = pl.ds(pl.multiple_of(first * capacity_rows, SUBLANES), group * capacity_rows)
+        wanted = req_ref[window]
+        found = lookup(table_ref[:, 0:rows], wanted >> 7, wanted & (LANES - 1))
+        ans_out[pl.ds(first, group)] = cut(found, capacity_rows)
+        return first, jnp.sum(found, axis=0, keepdims=True)
+
+    def reply(first, count):
+        for j in range(1, count + 1):
+            target = first + lax.rem(spot + j, group)
+            copy(2, ans_out.at[target], ans_in.at[me], target).start()
+
+    def step(turn, total):
+        first, part = answer(turn)
+        reply(first, group)
+        return total + part
+
+    total = lax.fori_loop(1, groups, step, jnp.zeros((1, LANES), f32))
+    first, part = answer(0)
+    reply(first, group - 1)
+    ans_in[me] = ans_out[me]
+    tot_out[0] = total + part
+    spread(4, tot_out, tot_in)
+
+    all_of(2, ans_in).wait_recv()
+    table_ref[:, 0:codes] = split_table(join(ans_in[...]))
+    for first in range(0, samp_rows, 32):
+        window = slice(first, first + 32)
+        probs_ref[window] = lookup(table_ref[:, 0:codes], code_ref[window], rank_ref[window])
+    all_of(4, tot_in).wait_recv()
+    all_of(3, his_in).wait_recv()
     hist_ref[...] = jnp.sum(his_in[...], axis=0)
     fid_ref[...] = jnp.sum(tot_in[...], axis=0)
 
-    for channel, into in enumerate((amp_in, req_in, wt_in, ans_in, his_in, tot_in)):
+    for channel, into in enumerate((amp_in, wt_in, ans_in, his_in, tot_in)):
         all_of(channel, into).wait_send()
 
 
 def finish(sizes, values, hist, totals, probs_ref, mine_ref, fid_ref):
-    amps_total, samples = sizes
-    bins, mine = float(hist.shape[0] * LANES), mine_ref.shape[1]
+    amps_total, samples, bins = sizes
+    mine = mine_ref.shape[1]
     start = lax.axis_index("dev") * mine
-    sums = jnp.sum(totals[...], axis=1, keepdims=True)
-    total, norm = sums[0:1], sums[1:2]
+    total = jnp.sum(totals[...], axis=1, keepdims=True)
+    norm = jnp.sum(hist[1:2], axis=1, keepdims=True)
     probs_ref[...] = amps_total * (values[...] / norm)
-    line = hist[pl.ds(start // LANES, 1)]
-    line = jnp.broadcast_to(line, (SUBLANES, LANES))
+    line = jnp.broadcast_to(hist[0:1], (SUBLANES, LANES))
     line = pltpu.roll(line, (LANES - start % LANES) % LANES, 1)
     mine_ref[...] = bins * (line[0:1, :mine] / norm)
     fid_ref[...] = amps_total * (total / norm) / samples - 1.0
@@ -490,33 +473,30 @@
         functools.partial(kernel, sizes),
         out_shape=(
             jax.ShapeDtypeStruct((samp_rows, LANES), f32),
-            jax.ShapeDtypeStruct((bin_rows, LANES), f32),
             jax.ShapeDtypeStruct((2, LANES), f32),
+            jax.ShapeDtypeStruct((1, LANES), f32),
         ),
         in_specs=[smem, smem, vmem, vmem, vmem],
         out_specs=(vmem, vmem, vmem),
         scratch_shapes=[
             pltpu.VMEM((devices, 2, depth, LANES), f32),
             pltpu.VMEM((devices, 2, depth, LANES), f32),
-            pltpu.VMEM((devices, depth, LANES), f32),
-            pltpu.VMEM((devices, depth, LANES), f32),
-            pltpu.VMEM((devices, capacity_rows, LANES), i32),
-            pltpu.VMEM((devices, capacity_rows, LANES), i32),
+            pltpu.VMEM((devices, depth + capacity_rows, LANES), f32),
+            pltpu.VMEM((devices, depth + capacity_rows, LANES), f32),
             pltpu.VMEM((devices, capacity_rows, LANES), f32),
             pltpu.VMEM((devices, capacity_rows, LANES), f32),
-            pltpu.VMEM((1, bin_rows, LANES), f32),
-            pltpu.VMEM((devices, bin_rows, LANES), f32),
-            pltpu.VMEM((1, 2, LANES), f32),
+            pltpu.VMEM((bin_rows, 2, LANES), f32),
             pltpu.VMEM((devices, 2, LANES), f32),
+            pltpu.VMEM((1, 1, LANES), f32),
+            pltpu.VMEM((devices, 1, LANES), f32),
             pltpu.VMEM((samp_rows, LANES), i32),
             pltpu.VMEM((samp_rows, LANES), i32),
+            pltpu.VMEM((codes, LANES), i32),
             pltpu.VMEM((2 * LANES, max(rows, codes)), bf16),
-            pltpu.VMEM((rows, LANES), f32),
-            pltpu.VMEM((codes, LANES), f32),
+            pltpu.VMEM((2, 2 * devices, 2 * devices), bf16),
             pltpu.VMEM((8, -(-angles.shape[0] // SUBLANES) * SUBLANES, LANES), f32),
-            pltpu.SemaphoreType.DMA((6,)),
-            pltpu.SemaphoreType.DMA((6,)),
-            pltpu.SemaphoreType.DMA((devices,)),
+            pltpu.SemaphoreType.DMA((5,)),
+            pltpu.SemaphoreType.DMA((5,)),
         ],
         compiler_params=pltpu.CompilerParams(collective_id=0, has_side_effects=True),
         name="circuit",
@@ -528,7 +508,9 @@
         sample_low.reshape(samp_rows, LANES),
     )
     probs, mine, fid = pl.pallas_call(
-        functools.partial(finish, (float(amps_local * devices), float(samp_local * devices))),
+        functools.partial(
+            finish, (float(amps_local * devices), float(samp_local * devices), float(bins))
+        ),
         out_shape=(
             jax.ShapeDtypeStruct((samp_rows, LANES), f32),
             jax.ShapeDtypeStruct((1, bins // devices), f32),

time: 65.2 us -> 42.8 us (0.66)
  Pallas kernels: 64.3 us -> 42 us
    pallas_call x1, Pallas kernels: 62.9 us -> 40.5 us  [shards(): pl.pallas_call(functools.partial(kernel, sizes), out_shape=(jax.ShapeDtyp...]
where the time goes in v1:
time: 42.8 us; the launch traced here: 42.6 us
  Pallas kernels  42 us (98%)
  between operations  0.64 us (1%)
    pallas_call x1, Pallas kernels, shards(): pl.pallas_call(functools.partial(kernel, sizes), out_shape=(jax.ShapeDtyp...  40.5 us
    pallas_call x1, Pallas kernels, shards(): pl.pallas_call(functools.partial(finish, (float(amps_local * devices), fl...  1.48 us

profile of v1, /device:TPU:1, one launch (start us, length us, event | category | flops | bytes accessed | tf_op | source)
XLA Modules:
  0.0 42.6 jit_solution(18100332271421279859)
XLA Ops:
  0.6 40.5 %circuit.1 = (f32[64,128]{1,0:T(8,128)}, f32[2,128]{1,0:T(2,128)}, f32[1,128]{1,0:T(1,128)}) custom-call(f32[3,22]{1,0:T(4,128)} %bitcast.15, s32[1,10]{1,0:T(1,128)} %bitcast.16, f32[512,128]{1,0:T(8,128)} %bitcast.12, s32[64,128]{1,0:T(8,128)} %bitcast.13, s32[64,128]{1,0:T(8,128)} %bitcast.14), custom_call_target="tpu_custom_call" | custom-call | tf_op jit(solution)/shard_map/circuit/pallas_call | solution.py:472
  41.1 1.5 %finish.1 = (f32[64,128]{1,0:T(8,128)}, f32[1,8]{1,0:T(1,128)}, f32[1,1]{1,0:T(1,128)}) custom-call(f32[64,128]{1,0:T(8,128)} %get-tuple-element.9.values, f32[2,128]{1,0:T(2,128)} %get-tuple-element.10.hist, f32[1,128]{1,0:T(1,128)} %get-tuple-element.11.totals), custom_call_target="tpu_custom_call" | custom-call | tf_op jit(solution)/shard_map/finish/pallas_call | solution.py:510

commit v2 on v1

--- a/solution.py
+++ b/solution.py
@@ -1,4 +1,5 @@
 import functools
+import itertools
 
 import jax
 import jax.numpy as jnp
@@ -9,6 +10,7 @@
 
 LANES = 128
 SUBLANES = 8
+TORUS = (4, 4, 4, 2)
 f32 = jnp.float32
 bf16 = jnp.bfloat16
 i32 = jnp.int32
@@ -168,13 +170,31 @@
     return jnp.concatenate(found, axis=0)
 
 
+def routes(me):
+    parts = []
+    rest = me
+    for size in reversed(TORUS):
+        parts.insert(0, lax.rem(rest, size))
+        rest = rest // size
+    scale = 1
+    tables = []
+    for part, size in zip(reversed(parts), reversed(TORUS)):
+        tables.insert(0, [lax.rem(part + step, size) * scale for step in range(size)])
+        scale *= size
+    steps = list(itertools.product(*[range(size) for size in TORUS]))
+    steps.sort(key=lambda step: -sum(min(d, n - d) for d, n in zip(step[:3], TORUS[:3])))
+    upper = {(a, b): tables[0][a] + tables[1][b] for a in range(TORUS[0]) for b in range(TORUS[1])}
+    lower = {(a, b): tables[2][a] + tables[3][b] for a in range(TORUS[2]) for b in range(TORUS[3])}
+    return [upper[step[:2]] + lower[step[2:]] for step in steps if any(step)]
+
+
 def kernel(
     sizes,
-    angles,
-    marg,
-    state,
-    owner_ref,
-    low_ref,
+    angles_hbm,
+    marg_hbm,
+    state_hbm,
+    owner_hbm,
+    low_hbm,
     probs_ref,
     hist_ref,
     fid_ref,
@@ -194,8 +214,14 @@
     table_ref,
     global_ref,
     gates,
+    angles,
+    marg,
+    state,
+    owner_ref,
+    low_ref,
     sends,
     recvs,
+    loads,
 ):
     devices, depth, capacity_rows, marg_count = sizes
     me = lax.axis_index("dev")
@@ -205,8 +231,21 @@
     local_bits = row_bits + 7
     codes = devices * capacity_rows
 
-    def peer(k):
-        return lax.rem(me + k, devices)
+    peers = routes(me)
+    inputs = [
+        pltpu.make_async_copy(src, dst, loads.at[n])
+        for n, (src, dst) in enumerate(
+            (
+                (angles_hbm, angles),
+                (state_hbm, state),
+                (owner_hbm, owner_ref),
+                (low_hbm, low_ref),
+                (marg_hbm, marg),
+            )
+        )
+    ]
+    for load in inputs:
+        load.start()
 
     def copy(channel, src, dst, target):
         return pltpu.make_async_remote_copy(
@@ -219,32 +258,27 @@
         )
 
     def scatter(channel, out, into):
-        @pl.loop(1, devices)
-        def _(k):
-            target = peer(k)
+        for target in peers:
             copy(channel, out.at[target], into.at[me], target).start()
-
         into[me] = out[me]
 
     def spread(channel, out, into):
-        @pl.loop(1, devices)
-        def _(k):
-            copy(channel, out.at[0], into.at[me], peer(k)).start()
-
+        for target in peers:
+            copy(channel, out.at[0], into.at[me], target).start()
         into[me] = out[0]
 
     def all_of(channel, into):
         many = into.at[pl.ds(0, devices - 1)]
-        return copy(channel, many, many, peer(1))
+        return copy(channel, many, many, peers[-1])
 
     barrier = pltpu.get_barrier_semaphore()
 
-    @pl.loop(1, devices)
-    def _(k):
+    for target in peers:
         pl.semaphore_signal(
-            barrier, inc=1, device_id=(peer(k),), device_id_type=pl.DeviceIdType.MESH
+            barrier, inc=1, device_id=(target,), device_id_type=pl.DeviceIdType.MESH
         )
 
+    inputs[0].wait()
     for e, entry in enumerate(gate_rows(angles, global_bits + local_bits)):
         gates[e] = entry
 
@@ -255,6 +289,7 @@
     mixed = jnp.concatenate(
         [jnp.concatenate([mr, mi], axis=1), jnp.concatenate([-mi, mr], axis=1)], axis=0
     )
+    inputs[1].wait()
     both = jnp.concatenate(
         [state[pl.ds(0, rows, stride=2)], state[pl.ds(1, rows, stride=2)]], axis=1
     )
@@ -277,6 +312,8 @@
     scatter(0, amp_out, amp_in)
 
     samp_rows = owner_ref.shape[0]
+    for load in inputs[2:]:
+        load.wait()
     owner = owner_ref[...]
     owner_ids = iota((devices, LANES), 0)
     chunks = samp_rows // 2
@@ -383,9 +420,7 @@
 
     bin_share = devices * LANES // bins
 
-    @pl.loop(1, devices)
-    def _(k):
-        target = peer(k)
+    for target in peers:
         copy(3, his_out.at[target // bin_share], his_in.at[me], target).start()
 
     his_in[me] = his_out[me // bin_share]
@@ -466,7 +501,6 @@
         marg_count,
     )
     vmem = pl.BlockSpec(memory_space=pltpu.VMEM)
-    smem = pl.BlockSpec(memory_space=pltpu.SMEM)
     codes = devices * capacity_rows
     bin_rows = bins // LANES
     values, hist, totals = pl.pallas_call(
@@ -476,7 +510,7 @@
             jax.ShapeDtypeStruct((2, LANES), f32),
             jax.ShapeDtypeStruct((1, LANES), f32),
         ),
-        in_specs=[smem, smem, vmem, vmem, vmem],
+        in_specs=[pl.BlockSpec(memory_space=pl.ANY)] * 5,
         out_specs=(vmem, vmem, vmem),
         scratch_shapes=[
             pltpu.VMEM((devices, 2, depth, LANES), f32),
@@ -495,6 +529,12 @@
             pltpu.VMEM((2 * LANES, max(rows, codes)), bf16),
             pltpu.VMEM((2, 2 * devices, 2 * devices), bf16),
             pltpu.VMEM((8, -(-angles.shape[0] // SUBLANES) * SUBLANES, LANES), f32),
+            pltpu.SMEM((angles.shape[1], angles.shape[0]), f32),
+            pltpu.SMEM((1, marg_count), i32),
+            pltpu.VMEM((2 * rows, LANES), f32),
+            pltpu.VMEM((samp_rows, LANES), i32),
+            pltpu.VMEM((samp_rows, LANES), i32),
+            pltpu.SemaphoreType.DMA((5,)),
             pltpu.SemaphoreType.DMA((5,)),
             pltpu.SemaphoreType.DMA((5,)),
         ],

time: 42.8 us -> 40.1 us (0.937)
  Pallas kernels: 42 us -> 39.3 us
    pallas_call x1, Pallas kernels: 40.5 us -> 37.8 us  [shards(): pl.pallas_call(functools.partial(kernel, sizes), out_shape=(jax.ShapeDtyp...]
where the time goes in v2:
time: 40.1 us; the launch traced here: 39.9 us
  Pallas kernels  39.3 us (98%)
  between operations  0.64 us (2%)
    pallas_call x1, Pallas kernels, shards(): pl.pallas_call(functools.partial(kernel, sizes), out_shape=(jax.ShapeDtyp...  37.8 us
    pallas_call x1, Pallas kernels, shards(): pl.pallas_call(functools.partial(finish, (float(amps_local * devices), fl...  1.48 us

profile of v2, /device:TPU:1, one launch (start us, length us, event | category | flops | bytes accessed | tf_op | source)
XLA Modules:
  0.0 39.9 jit_solution(8141092149164565744)
XLA Ops:
  0.6 37.8 %circuit.1 = (f32[64,128]{1,0:T(8,128)}, f32[2,128]{1,0:T(2,128)}, f32[1,128]{1,0:T(1,128)}) custom-call(f32[3,22]{1,0:T(4,128)} %bitcast.15, s32[1,10]{1,0:T(1,128)} %bitcast.16, f32[512,128]{1,0:T(8,128)} %bitcast.12, s32[64,128]{1,0:T(8,128)} %bitcast.13, s32[64,128]{1,0:T(8,128)} %bitcast.14), custom_call_target="tpu_custom_call" | custom-call | tf_op jit(solution)/shard_map/circuit/pallas_call | solution.py:506
  38.5 1.5 %finish.1 = (f32[64,128]{1,0:T(8,128)}, f32[1,8]{1,0:T(1,128)}, f32[1,1]{1,0:T(1,128)}) custom-call(f32[64,128]{1,0:T(8,128)} %get-tuple-element.9.values, f32[2,128]{1,0:T(2,128)} %get-tuple-element.10.hist, f32[1,128]{1,0:T(1,128)} %get-tuple-element.11.totals), custom_call_target="tpu_custom_call" | custom-call | tf_op jit(solution)/shard_map/finish/pallas_call | solution.py:550

commit v3 on v2

--- a/solution.py
+++ b/solution.py
@@ -170,6 +170,30 @@
     return jnp.concatenate(found, axis=0)
 
 
+def lookup_lanes(plain, upper, lower):
+    bits = plain.shape[0].bit_length() - 1
+    high = [((upper >> bit) & 1) == 1 for bit in range(bits)]
+
+    def pick(first, bit):
+        if bit < 0:
+            line = jnp.broadcast_to(plain[first : first + 1], (SUBLANES, LANES))
+            return jnp.take_along_axis(line, lower, axis=1, mode="promise_in_bounds")
+        zero = pick(first, bit - 1)
+        return jnp.where(high[bit], pick(first + (1 << bit), bit - 1), zero)
+
+    return pick(0, bits - 1)
+
+
+def lookup_both(table, plain, upper, lower, lanes):
+    dots = upper.shape[0] - lanes
+    found = [lookup(table, upper[:dots], lower[:dots])]
+    for first in range(dots, dots + lanes, SUBLANES):
+        part = slice(first, first + SUBLANES)
+        value = lookup_lanes(plain, upper[part], lower[part])
+        found.append(jnp.where(upper[part] >= 0, value, 0.0))
+    return jnp.concatenate(found, axis=0)
+
+
 def routes(me):
     parts = []
     rest = me
@@ -204,14 +228,14 @@
     wt_in,
     ans_out,
     ans_in,
-    his_out,
-    his_in,
+    his_ref,
     tot_out,
     tot_in,
     code_ref,
     rank_ref,
     req_ref,
     table_ref,
+    plain_ref,
     global_ref,
     gates,
     angles,
@@ -414,21 +438,19 @@
         folded = jnp.dot(split, lane_hot, preferred_element_type=f32)
         folded = folded[:rows] + folded[rows:]
         picked = jnp.where(row_code == bin_id - lane_part, folded, 0.0)
-        his_out[c, 0:1] = jnp.sum(picked, axis=0, keepdims=True)
+        his_ref[pl.ds(c, 1)] = jnp.sum(picked, axis=0, keepdims=True)
+
+    bin_share = devices * LANES // bins
     for c in range(bins // LANES):
-        his_out[c, 1:2] = norm_part
-
-    bin_share = devices * LANES // bins
-
-    for target in peers:
-        copy(3, his_out.at[target // bin_share], his_in.at[me], target).start()
-
-    his_in[me] = his_out[me // bin_share]
+        part = slice(c * bin_share, (c + 1) * bin_share)
+        ans_out[part, capacity_rows] = jnp.broadcast_to(his_ref[c : c + 1], (bin_share, LANES))
+    ans_out[:, capacity_rows + 1] = jnp.broadcast_to(norm_part, (devices, LANES))
 
     all_of(1, wt_in).wait_recv()
-    table_ref[:, 0:rows] = split_table(join(wt_in[:, 0:depth]))
+    plain_ref[0:rows] = join(wt_in[:, 0:depth])
+    table_ref[:, 0:rows] = split_table(plain_ref[0:rows])
     req_ref[...] = join(wt_in[:, depth:]).astype(i32)
-    group = 32 // capacity_rows
+    group = 128 // capacity_rows
     groups = devices // group
     mine, spot = me // group, me % group
 
@@ -436,8 +458,10 @@
         first = lax.rem(mine + turn, groups) * group
         window = pl.ds(pl.multiple_of(first * capacity_rows, SUBLANES), group * capacity_rows)
         wanted = req_ref[window]
-        found = lookup(table_ref[:, 0:rows], wanted >> 7, wanted & (LANES - 1))
-        ans_out[pl.ds(first, group)] = cut(found, capacity_rows)
+        found = lookup_both(
+            table_ref[:, 0:rows], plain_ref.at[0:rows], wanted >> 7, wanted & (LANES - 1), 48
+        )
+        ans_out[pl.ds(first, group), 0:capacity_rows] = cut(found, capacity_rows)
         return first, jnp.sum(found, axis=0, keepdims=True)
 
     def reply(first, count):
@@ -455,19 +479,21 @@
     reply(first, group - 1)
     ans_in[me] = ans_out[me]
     tot_out[0] = total + part
-    spread(4, tot_out, tot_in)
+    spread(3, tot_out, tot_in)
 
     all_of(2, ans_in).wait_recv()
-    table_ref[:, 0:codes] = split_table(join(ans_in[...]))
+    plain_ref[0:codes] = join(ans_in[:, 0:capacity_rows])
+    table_ref[:, 0:codes] = split_table(plain_ref[0:codes])
     for first in range(0, samp_rows, 32):
         window = slice(first, first + 32)
-        probs_ref[window] = lookup(table_ref[:, 0:codes], code_ref[window], rank_ref[window])
-    all_of(4, tot_in).wait_recv()
-    all_of(3, his_in).wait_recv()
-    hist_ref[...] = jnp.sum(his_in[...], axis=0)
+        probs_ref[window] = lookup_both(
+            table_ref[:, 0:codes], plain_ref.at[0:codes], code_ref[window], rank_ref[window], 8
+        )
+    hist_ref[...] = jnp.sum(ans_in[:, capacity_rows:], axis=0)
+    all_of(3, tot_in).wait_recv()
     fid_ref[...] = jnp.sum(tot_in[...], axis=0)
 
-    for channel, into in enumerate((amp_in, wt_in, ans_in, his_in, tot_in)):
+    for channel, into in enumerate((amp_in, wt_in, ans_in, tot_in)):
         all_of(channel, into).wait_send()
 
 
@@ -510,23 +536,23 @@
             jax.ShapeDtypeStruct((2, LANES), f32),
             jax.ShapeDtypeStruct((1, LANES), f32),
         ),
-        in_specs=[pl.BlockSpec(memory_space=pl.ANY)] * 5,
+        in_specs=[pl.BlockSpec(memory_space=pltpu.HBM)] * 5,
         out_specs=(vmem, vmem, vmem),
         scratch_shapes=[
             pltpu.VMEM((devices, 2, depth, LANES), f32),
             pltpu.VMEM((devices, 2, depth, LANES), f32),
             pltpu.VMEM((devices, depth + capacity_rows, LANES), f32),
             pltpu.VMEM((devices, depth + capacity_rows, LANES), f32),
-            pltpu.VMEM((devices, capacity_rows, LANES), f32),
-            pltpu.VMEM((devices, capacity_rows, LANES), f32),
-            pltpu.VMEM((bin_rows, 2, LANES), f32),
-            pltpu.VMEM((devices, 2, LANES), f32),
+            pltpu.VMEM((devices, capacity_rows + 2, LANES), f32),
+            pltpu.VMEM((devices, capacity_rows + 2, LANES), f32),
+            pltpu.VMEM((bin_rows, LANES), f32),
             pltpu.VMEM((1, 1, LANES), f32),
             pltpu.VMEM((devices, 1, LANES), f32),
             pltpu.VMEM((samp_rows, LANES), i32),
             pltpu.VMEM((samp_rows, LANES), i32),
             pltpu.VMEM((codes, LANES), i32),
             pltpu.VMEM((2 * LANES, max(rows, codes)), bf16),
+            pltpu.VMEM((max(rows, codes), LANES), f32),
             pltpu.VMEM((2, 2 * devices, 2 * devices), bf16),
             pltpu.VMEM((8, -(-angles.shape[0] // SUBLANES) * SUBLANES, LANES), f32),
             pltpu.SMEM((angles.shape[1], angles.shape[0]), f32),
@@ -534,18 +560,20 @@
             pltpu.VMEM((2 * rows, LANES), f32),
             pltpu.VMEM((samp_rows, LANES), i32),
             pltpu.VMEM((samp_rows, LANES), i32),
-            pltpu.SemaphoreType.DMA((5,)),
-            pltpu.SemaphoreType.DMA((5,)),
+            pltpu.SemaphoreType.DMA((4,)),
+            pltpu.SemaphoreType.DMA((4,)),
             pltpu.SemaphoreType.DMA((5,)),
         ],
-        compiler_params=pltpu.CompilerParams(collective_id=0, has_side_effects=True),
+        compiler_params=pltpu.CompilerParams(
+            collective_id=0, has_side_effects=True, vmem_limit_bytes=24 << 20
+        ),
         name="circuit",
     )(
-        angles.T,
-        marginal_qubits.reshape(1, marg_count),
-        state.reshape(2, rows, LANES).transpose(1, 0, 2).reshape(2 * rows, LANES),
-        sample_high.reshape(samp_rows, LANES),
-        sample_low.reshape(samp_rows, LANES),
+        pltpu.with_memory_space_constraint(angles.T, pltpu.HBM),
+        pltpu.with_memory_space_constraint(marginal_qubits.reshape(1, marg_count), pltpu.HBM),
+        pltpu.with_memory_space_constraint(state.reshape(2, rows, LANES).transpose(1, 0, 2).reshape(2 * rows, LANES), pltpu.HBM),
+        pltpu.with_memory_space_constraint(sample_high.reshape(samp_rows, LANES), pltpu.HBM),
+        pltpu.with_memory_space_constraint(sample_low.reshape(samp_rows, LANES), pltpu.HBM),
     )
     probs, mine, fid = pl.pallas_call(
         functools.partial(
@@ -558,6 +586,7 @@
         ),
         in_specs=[vmem, vmem, vmem],
         out_specs=(vmem, vmem, vmem),
+        compiler_params=pltpu.CompilerParams(vmem_limit_bytes=1 << 20),
         name="finish",
     )(values, hist, totals)
     return probs.reshape(samp_local), mine.reshape(bins // devices), fid.reshape(())

time: 40.1 us -> 37.6 us (0.938)
  Pallas kernels: 39.3 us -> 36.8 us
    pallas_call x1, Pallas kernels: 37.8 us -> 36.1 us  [shards(): pl.pallas_call(functools.partial(kernel, sizes), out_shape=(jax.ShapeDtyp...]
    pallas_call x1, Pallas kernels: 1.48 us -> 0.7 us  [shards(): pl.pallas_call(functools.partial(finish, (float(amps_local * devices), fl...]
where the time goes in v3:
time: 37.6 us; the launch traced here: 37.5 us
  Pallas kernels  36.8 us (98%)
  between operations  0.64 us (2%)
    pallas_call x1, Pallas kernels, shards(): pl.pallas_call(functools.partial(kernel, sizes), out_shape=(jax.ShapeDtyp...  36.1 us

profile of v3, /device:TPU:1, one launch (start us, length us, event | category | flops | bytes accessed | tf_op | source)
XLA Modules:
  0.0 37.5 jit_solution(10302354458307084896)
XLA Ops:
  0.6 36.1 %circuit.1 = (f32[64,128]{1,0:T(8,128)S(1)}, f32[2,128]{1,0:T(2,128)S(1)}, f32[1,128]{1,0:T(1,128)S(1)}) custom-call(f32[3,22]{1,0:T(4,128)} %bitcast.15, s32[1,10]{1,0:T(1,128)} %bitcast.16, f32[512,128]{1,0:T(8,128)} %bitcast.12, s32[64,128]{1,0:T(8,128)} %bitcast.13, s32[64,128]{1,0:T(8,128)} %bitcast.14), custom_call_target="tpu_custom_call" | custom-call | tf_op jit(solution)/shard_map/circuit/pallas_call | solution.py:532
  36.8 0.7 %finish.1 = (f32[64,128]{1,0:T(8,128)}, f32[1,8]{1,0:T(1,128)}, f32[1,1]{1,0:T(1,128)}) custom-call(f32[64,128]{1,0:T(8,128)S(1)} %get-tuple-element.9.values, f32[2,128]{1,0:T(2,128)S(1)} %get-tuple-element.10.hist, f32[1,128]{1,0:T(1,128)S(1)} %get-tuple-element.11.totals), custom_call_target="tpu_custom_call" | custom-call | tf_op jit(solution)/shard_map/finish/pallas_call | solution.py:578

commit v4 on v3

--- a/solution.py
+++ b/solution.py
@@ -136,6 +136,14 @@
 def halves(x):
     top = x.astype(bf16)
     return top, (x - top.astype(f32)).astype(bf16)
+
+
+def marked(row, value, count):
+    shape = (2 * SUBLANES, LANES)
+    wide = jnp.broadcast_to(row.astype(f32), shape).astype(bf16)
+    value = jnp.broadcast_to(value.astype(f32), shape).astype(bf16)
+    ids = iota((count, LANES), 0).astype(f32).astype(bf16).reshape(count // 16, 16, LANES)
+    return jnp.where(ids == wide[None], value[None], jnp.zeros((), bf16)).reshape(count, LANES)
 
 
 def one_hot(row, count):
@@ -226,9 +234,12 @@
     amp_in,
     wt_out,
     wt_in,
+    req_out,
+    req_in,
     ans_out,
     ans_in,
-    his_ref,
+    his_out,
+    his_in,
     tot_out,
     tot_in,
     code_ref,
@@ -341,8 +352,7 @@
     owner = owner_ref[...]
     owner_ids = iota((devices, LANES), 0)
     chunks = samp_rows // 2
-    hot_rows = [(owner_ids == owner[r : r + 1]) for r in range(samp_rows)]
-    pieces = [h.astype(f32).astype(bf16) for h in hot_rows]
+    pieces = [one_hot(owner[r : r + 1], devices) for r in range(samp_rows)]
     stacked = jnp.concatenate(
         [jnp.concatenate(pieces[2 * c : 2 * c + 2], axis=1) for c in range(chunks)], axis=0
     )
@@ -360,33 +370,30 @@
             ranks.append(jnp.sum(jnp.where(mine, spot, 0.0), axis=0, keepdims=True))
         before = before + block[:, 2 * LANES :]
     ranking = jnp.concatenate(ranks, axis=0).astype(i32)
-    code_ref[...] = owner * capacity_rows + (ranking >> 7)
-    rank_ref[...] = ranking & (LANES - 1)
-
-    lane_ids = iota((LANES, LANES), 0)
-    steps = samp_rows // SUBLANES
-
-    def place(t, placed):
-        window = pl.ds(pl.multiple_of(t * SUBLANES, SUBLANES), SUBLANES)
-        code, rank, low = code_ref[window], rank_ref[window], low_ref[window] + 1
-        low_top = (low >> 8).astype(f32)
-        low_rest = (low & 255).astype(f32)
-        hot = jnp.concatenate([one_hot(code[r : r + 1], codes) for r in range(SUBLANES)], axis=1)
-        tops, rests = [], []
-        for r in range(SUBLANES):
-            here = lane_ids == rank[r : r + 1]
-            tops.append(jnp.where(here, low_top[r : r + 1], 0.0).astype(bf16))
-            rests.append(jnp.where(here, low_rest[r : r + 1], 0.0).astype(bf16))
-        values = jnp.concatenate(
-            [jnp.concatenate(tops, axis=1), jnp.concatenate(rests, axis=1)], axis=0
+    code = owner * capacity_rows + (ranking >> 7)
+    rank = ranking & (LANES - 1)
+    code_ref[...] = code
+    rank_ref[...] = rank
+
+    low = low_ref[...] + 1
+    tops, rests = low >> 8, low & 255
+    placed = jnp.zeros((codes, 2 * LANES), f32)
+    for first in range(0, samp_rows, 16):
+        line = [slice(r, r + 1) for r in range(first, first + 16)]
+        hot = jnp.concatenate([one_hot(code[r], codes) for r in line], axis=1)
+        values = [
+            jnp.concatenate([marked(rank[r], part[r], LANES) for r in line], axis=1)
+            for part in (tops, rests)
+        ]
+        placed = placed + lax.dot_general(
+            hot,
+            jnp.concatenate(values, axis=0),
+            (((1,), (1,)), ((), ())),
+            preferred_element_type=f32,
         )
-        return placed + lax.dot_general(
-            hot, values, (((1,), (1,)), ((), ())), preferred_element_type=f32
-        )
-
-    placed = lax.fori_loop(0, steps, place, jnp.zeros((codes, 2 * LANES), f32))
-    wanted = placed[:, :LANES] * 256.0 + placed[:, LANES:] - 1.0
-    wt_out[:, depth:] = cut(wanted, capacity_rows)
+    wanted = (placed[:, :LANES] * 256.0 + placed[:, LANES:]).astype(i32) - 1
+    req_out[...] = cut(wanted, capacity_rows)
+    scatter(5, req_out, req_in)
 
     all_of(0, amp_in).wait_recv()
     both = jnp.concatenate(
@@ -438,19 +445,19 @@
         folded = jnp.dot(split, lane_hot, preferred_element_type=f32)
         folded = folded[:rows] + folded[rows:]
         picked = jnp.where(row_code == bin_id - lane_part, folded, 0.0)
-        his_ref[pl.ds(c, 1)] = jnp.sum(picked, axis=0, keepdims=True)
+        his_out[c] = jnp.sum(picked, axis=0, keepdims=True)
 
     bin_share = devices * LANES // bins
-    for c in range(bins // LANES):
-        part = slice(c * bin_share, (c + 1) * bin_share)
-        ans_out[part, capacity_rows] = jnp.broadcast_to(his_ref[c : c + 1], (bin_share, LANES))
-    ans_out[:, capacity_rows + 1] = jnp.broadcast_to(norm_part, (devices, LANES))
-
+    for target in peers:
+        copy(4, his_out.at[target // bin_share], his_in.at[me], target).start()
+    his_in[me] = his_out[me // bin_share]
+
+    all_of(5, req_in).wait_recv()
+    req_ref[...] = join(req_in[...])
     all_of(1, wt_in).wait_recv()
-    plain_ref[0:rows] = join(wt_in[:, 0:depth])
+    plain_ref[0:rows] = join(wt_in[...])
     table_ref[:, 0:rows] = split_table(plain_ref[0:rows])
-    req_ref[...] = join(wt_in[:, depth:]).astype(i32)
-    group = 128 // capacity_rows
+    group = 64 // capacity_rows
     groups = devices // group
     mine, spot = me // group, me % group
 
@@ -459,9 +466,9 @@
         window = pl.ds(pl.multiple_of(first * capacity_rows, SUBLANES), group * capacity_rows)
         wanted = req_ref[window]
         found = lookup_both(
-            table_ref[:, 0:rows], plain_ref.at[0:rows], wanted >> 7, wanted & (LANES - 1), 48
+            table_ref[:, 0:rows], plain_ref.at[0:rows], wanted >> 7, wanted & (LANES - 1), 24
         )
-        ans_out[pl.ds(first, group), 0:capacity_rows] = cut(found, capacity_rows)
+        ans_out[pl.ds(first, group)] = cut(found, capacity_rows)
         return first, jnp.sum(found, axis=0, keepdims=True)
 
     def reply(first, count):
@@ -469,31 +476,35 @@
             target = first + lax.rem(spot + j, group)
             copy(2, ans_out.at[target], ans_in.at[me], target).start()
 
-    def step(turn, total):
-        first, part = answer(turn)
-        reply(first, group)
-        return total + part
-
-    total = lax.fori_loop(1, groups, step, jnp.zeros((1, LANES), f32))
-    first, part = answer(0)
-    reply(first, group - 1)
+    total = jnp.zeros((1, LANES), f32)
+    before = None
+    for turn in [*range(1, groups), 0]:
+        if before is not None:
+            reply(before, group)
+        before, part = answer(turn)
+        total = total + part
+    reply(before, group - 1)
+    half = iota((1, LANES), 1) < LANES // 2
+    packed = [jnp.broadcast_to(x, (SUBLANES, LANES)) for x in (total, norm_part)]
+    packed = [x + pltpu.roll(x, LANES // 2, 1) for x in packed]
+    tot_out[0] = jnp.where(half, packed[0][0:1], packed[1][0:1])
+    spread(3, tot_out, tot_in)
     ans_in[me] = ans_out[me]
-    tot_out[0] = total + part
-    spread(3, tot_out, tot_in)
 
     all_of(2, ans_in).wait_recv()
-    plain_ref[0:codes] = join(ans_in[:, 0:capacity_rows])
+    plain_ref[0:codes] = join(ans_in[...])
     table_ref[:, 0:codes] = split_table(plain_ref[0:codes])
     for first in range(0, samp_rows, 32):
         window = slice(first, first + 32)
         probs_ref[window] = lookup_both(
             table_ref[:, 0:codes], plain_ref.at[0:codes], code_ref[window], rank_ref[window], 8
         )
-    hist_ref[...] = jnp.sum(ans_in[:, capacity_rows:], axis=0)
+    all_of(4, his_in).wait_recv()
+    hist_ref[...] = jnp.sum(his_in[...], axis=0)
     all_of(3, tot_in).wait_recv()
     fid_ref[...] = jnp.sum(tot_in[...], axis=0)
 
-    for channel, into in enumerate((amp_in, wt_in, ans_in, tot_in)):
+    for channel, into in enumerate((amp_in, wt_in, ans_in, tot_in, his_in, req_in)):
         all_of(channel, into).wait_send()
 
 
@@ -501,8 +512,10 @@
     amps_total, samples, bins = sizes
     mine = mine_ref.shape[1]
     start = lax.axis_index("dev") * mine
-    total = jnp.sum(totals[...], axis=1, keepdims=True)
-    norm = jnp.sum(hist[1:2], axis=1, keepdims=True)
+    line = totals[...]
+    half = iota(line.shape, 1) < LANES // 2
+    total = jnp.sum(jnp.where(half, line, 0.0), axis=1, keepdims=True)
+    norm = jnp.sum(jnp.where(half, 0.0, line), axis=1, keepdims=True)
     probs_ref[...] = amps_total * (values[...] / norm)
     line = jnp.broadcast_to(hist[0:1], (SUBLANES, LANES))
     line = pltpu.roll(line, (LANES - start % LANES) % LANES, 1)
@@ -533,7 +546,7 @@
         functools.partial(kernel, sizes),
         out_shape=(
             jax.ShapeDtypeStruct((samp_rows, LANES), f32),
-            jax.ShapeDtypeStruct((2, LANES), f32),
+            jax.ShapeDtypeStruct((1, LANES), f32),
             jax.ShapeDtypeStruct((1, LANES), f32),
         ),
         in_specs=[pl.BlockSpec(memory_space=pltpu.HBM)] * 5,
@@ -541,11 +554,14 @@
         scratch_shapes=[
             pltpu.VMEM((devices, 2, depth, LANES), f32),
             pltpu.VMEM((devices, 2, depth, LANES), f32),
-            pltpu.VMEM((devices, depth + capacity_rows, LANES), f32),
-            pltpu.VMEM((devices, depth + capacity_rows, LANES), f32),
-            pltpu.VMEM((devices, capacity_rows + 2, LANES), f32),
-            pltpu.VMEM((devices, capacity_rows + 2, LANES), f32),
-            pltpu.VMEM((bin_rows, LANES), f32),
+            pltpu.VMEM((devices, depth, LANES), f32),
+            pltpu.VMEM((devices, depth, LANES), f32),
+            pltpu.VMEM((devices, capacity_rows, LANES), i32),
+            pltpu.VMEM((devices, capacity_rows, LANES), i32),
+            pltpu.VMEM((devices, capacity_rows, LANES), f32),
+            pltpu.VMEM((devices, capacity_rows, LANES), f32),
+            pltpu.VMEM((bin_rows, 1, LANES), f32),
+            pltpu.VMEM((devices, 1, LANES), f32),
             pltpu.VMEM((1, 1, LANES), f32),
             pltpu.VMEM((devices, 1, LANES), f32),
             pltpu.VMEM((samp_rows, LANES), i32),
@@ -560,8 +576,8 @@
             pltpu.VMEM((2 * rows, LANES), f32),
             pltpu.VMEM((samp_rows, LANES), i32),
             pltpu.VMEM((samp_rows, LANES), i32),
-            pltpu.SemaphoreType.DMA((4,)),
-            pltpu.SemaphoreType.DMA((4,)),
+            pltpu.SemaphoreType.DMA((6,)),
+            pltpu.SemaphoreType.DMA((6,)),
             pltpu.SemaphoreType.DMA((5,)),
         ],
         compiler_params=pltpu.CompilerParams(

time: 37.6 us -> 36.4 us (0.968)
  Pallas kernels: 36.8 us -> 35.6 us
    pallas_call x1, Pallas kernels: 36.1 us -> 34.9 us  [shards(): pl.pallas_call(functools.partial(kernel, sizes), out_shape=(jax.ShapeDtyp...]
where the time goes in v4:
time: 36.4 us; the launch traced here: 36.3 us
  Pallas kernels  35.6 us (98%)
  between operations  0.64 us (2%)
    pallas_call x1, Pallas kernels, shards(): pl.pallas_call(functools.partial(kernel, sizes), out_shape=(jax.ShapeDtyp...  34.9 us

profile of v4, /device:TPU:1, one launch (start us, length us, event | category | flops | bytes accessed | tf_op | source)
XLA Modules:
  0.0 36.3 jit_solution(11754778010656804589)
XLA Ops:
  0.6 34.9 %circuit.1 = (f32[64,128]{1,0:T(8,128)S(1)}, f32[1,128]{1,0:T(1,128)S(1)}, f32[1,128]{1,0:T(1,128)S(1)}) custom-call(f32[3,22]{1,0:T(4,128)} %bitcast.15, s32[1,10]{1,0:T(1,128)} %bitcast.16, f32[512,128]{1,0:T(8,128)} %bitcast.12, s32[64,128]{1,0:T(8,128)} %bitcast.13, s32[64,128]{1,0:T(8,128)} %bitcast.14), custom_call_target="tpu_custom_call" | custom-call | tf_op jit(solution)/shard_map/circuit/pallas_call | solution.py:545
  35.6 0.7 %finish.1 = (f32[64,128]{1,0:T(8,128)}, f32[1,8]{1,0:T(1,128)}, f32[1,1]{1,0:T(1,128)}) custom-call(f32[64,128]{1,0:T(8,128)S(1)} %get-tuple-element.9.values, f32[1,128]{1,0:T(1,128)S(1)} %get-tuple-element.10.hist, f32[1,128]{1,0:T(1,128)S(1)} %get-tuple-element.11.totals), custom_call_target="tpu_custom_call" | custom-call | tf_op jit(solution)/shard_map/finish/pallas_call | solution.py:594

commit v5 on v4

--- a/solution.py
+++ b/solution.py
@@ -159,22 +159,30 @@
     return jnp.concatenate([top, rest], axis=0)
 
 
+def pick_lane(value, lower):
+    value = value.reshape(LANES // SUBLANES, SUBLANES, LANES)
+    low = jnp.broadcast_to(lower, (SUBLANES, LANES))
+    for bit in (6, 5, 4, 3):
+        half = value.shape[0] // 2
+        value = jnp.where((((low >> bit) & 1) == 1)[None], value[half:], value[:half])
+    sub = iota((SUBLANES, LANES), 0)
+    value = jnp.where(sub == (low & (SUBLANES - 1)), value[0], 0.0)
+    return jnp.sum(value, axis=0, keepdims=True)
+
+
+def rows_dot(table, upper):
+    count = table.shape[1]
+    hot = [one_hot(upper[r : r + 1], count) for r in range(upper.shape[0])]
+    both = jnp.dot(table, jnp.concatenate(hot, axis=1), preferred_element_type=f32)
+    return both[:LANES] + both[LANES:]
+
+
 def lookup(table, upper, lower):
-    rows = upper.shape[0]
-    count = table.shape[1]
-    hot = jnp.concatenate([one_hot(upper[r : r + 1], count) for r in range(rows)], axis=1)
-    both = jnp.dot(table, hot, preferred_element_type=f32)
-    sub = iota((SUBLANES, LANES), 0)
-    found = []
-    for r in range(rows):
-        part = slice(r * LANES, (r + 1) * LANES)
-        value = (both[:LANES, part] + both[LANES:, part]).reshape(LANES // SUBLANES, SUBLANES, LANES)
-        low = jnp.broadcast_to(lower[r : r + 1], (SUBLANES, LANES))
-        for bit in (6, 5, 4, 3):
-            half = value.shape[0] // 2
-            value = jnp.where((((low >> bit) & 1) == 1)[None], value[half:], value[:half])
-        value = jnp.where(sub == (low & (SUBLANES - 1)), value[0], 0.0)
-        found.append(jnp.sum(value, axis=0, keepdims=True))
+    both = rows_dot(table, upper)
+    found = [
+        pick_lane(both[:, r * LANES : (r + 1) * LANES], lower[r : r + 1])
+        for r in range(upper.shape[0])
+    ]
     return jnp.concatenate(found, axis=0)
 
 
@@ -247,6 +255,8 @@
     req_ref,
     table_ref,
     plain_ref,
+    both_ref,
+    side_ref,
     global_ref,
     gates,
     angles,
@@ -457,17 +467,36 @@
     all_of(1, wt_in).wait_recv()
     plain_ref[0:rows] = join(wt_in[...])
     table_ref[:, 0:rows] = split_table(plain_ref[0:rows])
-    group = 64 // capacity_rows
+    group = 32 // capacity_rows
     groups = devices // group
     mine, spot = me // group, me % group
 
-    def answer(turn):
+    dots = 32 - 8
+
+    def place_of(turn):
         first = lax.rem(mine + turn, groups) * group
-        window = pl.ds(pl.multiple_of(first * capacity_rows, SUBLANES), group * capacity_rows)
-        wanted = req_ref[window]
-        found = lookup_both(
-            table_ref[:, 0:rows], plain_ref.at[0:rows], wanted >> 7, wanted & (LANES - 1), 24
-        )
+        start = pl.multiple_of(first * capacity_rows, SUBLANES)
+        return first, req_ref[pl.ds(start, group * capacity_rows)]
+
+    def begin(turn, slot):
+        _, wanted = place_of(turn)
+        upper, lower = wanted >> 7, wanted & (LANES - 1)
+        both_ref[slot] = rows_dot(table_ref[:, 0:rows], upper[:dots])
+        for first in range(dots, 32, SUBLANES):
+            part = slice(first, first + SUBLANES)
+            value = lookup_lanes(plain_ref.at[0:rows], upper[part], lower[part])
+            side_ref[slot, first - dots : first - dots + SUBLANES] = jnp.where(
+                upper[part] >= 0, value, 0.0
+            )
+
+    def answer(turn, slot):
+        first, wanted = place_of(turn)
+        lower = wanted & (LANES - 1)
+        found = [
+            pick_lane(both_ref[slot, :, r * LANES : (r + 1) * LANES], lower[r : r + 1])
+            for r in range(dots)
+        ]
+        found = jnp.concatenate([*found, side_ref[slot]], axis=0)
         ans_out[pl.ds(first, group)] = cut(found, capacity_rows)
         return first, jnp.sum(found, axis=0, keepdims=True)
 
@@ -477,12 +506,15 @@
             copy(2, ans_out.at[target], ans_in.at[me], target).start()
 
     total = jnp.zeros((1, LANES), f32)
-    before = None
-    for turn in [*range(1, groups), 0]:
-        if before is not None:
+    turns = [*range(1, groups), 0]
+    begin(turns[0], 0)
+    for n, turn in enumerate(turns):
+        if n + 1 < groups:
+            begin(turns[n + 1], (n + 1) % 2)
+        before, extra = answer(turn, n % 2)
+        total = total + extra
+        if n + 1 < groups:
             reply(before, group)
-        before, part = answer(turn)
-        total = total + part
     reply(before, group - 1)
     half = iota((1, LANES), 1) < LANES // 2
     packed = [jnp.broadcast_to(x, (SUBLANES, LANES)) for x in (total, norm_part)]
@@ -569,6 +601,8 @@
             pltpu.VMEM((codes, LANES), i32),
             pltpu.VMEM((2 * LANES, max(rows, codes)), bf16),
             pltpu.VMEM((max(rows, codes), LANES), f32),
+            pltpu.VMEM((2, LANES, (32 - 8) * LANES), f32),
+            pltpu.VMEM((2, 8, LANES), f32),
             pltpu.VMEM((2, 2 * devices, 2 * devices), bf16),
             pltpu.VMEM((8, -(-angles.shape[0] // SUBLANES) * SUBLANES, LANES), f32),
             pltpu.SMEM((angles.shape[1], angles.shape[0]), f32),

time: 36.4 us -> 35.3 us (0.970)
  Pallas kernels: 35.6 us -> 34.5 us
    pallas_call x1, Pallas kernels: 34.9 us -> 33.8 us  [shards(): pl.pallas_call(functools.partial(kernel, sizes), out_shape=(jax.ShapeDtyp...]
where the time goes in v5:
time: 35.3 us; the launch traced here: 35.2 us
  Pallas kernels  34.5 us (98%)
  between operations  0.64 us (2%)
    pallas_call x1, Pallas kernels, shards(): pl.pallas_call(functools.partial(kernel, sizes), out_shape=(jax.ShapeDtyp...  33.8 us
    pallas_call x1, Pallas kernels, shards(): pl.pallas_call(functools.partial(finish, (float(amps_local * devices), fl...  0.71 us

profile of v5, /device:TPU:1, one launch (start us, length us, event | category | flops | bytes accessed | tf_op | source)
XLA Modules:
  0.0 35.2 jit_solution(8576940785152628725)
XLA Ops:
  0.6 33.8 %circuit.1 = (f32[64,128]{1,0:T(8,128)S(1)}, f32[1,128]{1,0:T(1,128)S(1)}, f32[1,128]{1,0:T(1,128)S(1)}) custom-call(f32[3,22]{1,0:T(4,128)} %bitcast.15, s32[1,10]{1,0:T(1,128)} %bitcast.16, f32[512,128]{1,0:T(8,128)} %bitcast.12, s32[64,128]{1,0:T(8,128)} %bitcast.13, s32[64,128]{1,0:T(8,128)} %bitcast.14), custom_call_target="tpu_custom_call" | custom-call | tf_op jit(solution)/shard_map/circuit/pallas_call | solution.py:577
  34.5 0.7 %finish.1 = (f32[64,128]{1,0:T(8,128)}, f32[1,8]{1,0:T(1,128)}, f32[1,1]{1,0:T(1,128)}) custom-call(f32[64,128]{1,0:T(8,128)S(1)} %get-tuple-element.9.values, f32[1,128]{1,0:T(1,128)S(1)} %get-tuple-element.10.hist, f32[1,128]{1,0:T(1,128)S(1)} %get-tuple-element.11.totals), custom_call_target="tpu_custom_call" | custom-call | tf_op jit(solution)/shard_map/finish/pallas_call | solution.py:628

commit v6 on v5

--- a/solution.py
+++ b/solution.py
@@ -1,5 +1,6 @@
 import functools
 import itertools
+import random
 
 import jax
 import jax.numpy as jnp
@@ -221,11 +222,12 @@
     for part, size in zip(reversed(parts), reversed(TORUS)):
         tables.insert(0, [lax.rem(part + step, size) * scale for step in range(size)])
         scale *= size
-    steps = list(itertools.product(*[range(size) for size in TORUS]))
+    steps = [step for step in itertools.product(*[range(size) for size in TORUS]) if any(step)]
+    random.Random(1).shuffle(steps)
     steps.sort(key=lambda step: -sum(min(d, n - d) for d, n in zip(step[:3], TORUS[:3])))
     upper = {(a, b): tables[0][a] + tables[1][b] for a in range(TORUS[0]) for b in range(TORUS[1])}
     lower = {(a, b): tables[2][a] + tables[3][b] for a in range(TORUS[2]) for b in range(TORUS[3])}
-    return [upper[step[:2]] + lower[step[2:]] for step in steps if any(step)]
+    return [upper[step[:2]] + lower[step[2:]] for step in steps]
 
 
 def kernel(

time: 35.3 us -> 35 us (level)
  no operation moved by 1% of the time
where the time goes in v6:
time: 35 us; the launch traced here: 34.9 us
  Pallas kernels  34.2 us (98%)
  between operations  0.64 us (2%)
    pallas_call x1, Pallas kernels, shards(): pl.pallas_call(functools.partial(kernel, sizes), out_shape=(jax.ShapeDtyp...  33.5 us
    pallas_call x1, Pallas kernels, shards(): pl.pallas_call(functools.partial(finish, (float(amps_local * devices), fl...  0.71 us

profile of v6, /device:TPU:1, one launch (start us, length us, event | category | flops | bytes accessed | tf_op | source)
XLA Modules:
  0.0 34.9 jit_solution(16389471804479497480)
XLA Ops:
  0.6 33.5 %circuit.1 = (f32[64,128]{1,0:T(8,128)S(1)}, f32[1,128]{1,0:T(1,128)S(1)}, f32[1,128]{1,0:T(1,128)S(1)}) custom-call(f32[3,22]{1,0:T(4,128)} %bitcast.15, s32[1,10]{1,0:T(1,128)} %bitcast.16, f32[512,128]{1,0:T(8,128)} %bitcast.12, s32[64,128]{1,0:T(8,128)} %bitcast.13, s32[64,128]{1,0:T(8,128)} %bitcast.14), custom_call_target="tpu_custom_call" | custom-call | tf_op jit(solution)/shard_map/circuit/pallas_call | solution.py:579
  34.2 0.7 %finish.1 = (f32[64,128]{1,0:T(8,128)}, f32[1,8]{1,0:T(1,128)}, f32[1,1]{1,0:T(1,128)}) custom-call(f32[64,128]{1,0:T(8,128)S(1)} %get-tuple-element.9.values, f32[1,128]{1,0:T(1,128)S(1)} %get-tuple-element.10.hist, f32[1,128]{1,0:T(1,128)S(1)} %get-tuple-element.11.totals), custom_call_target="tpu_custom_call" | custom-call | tf_op jit(solution)/shard_map/finish/pallas_call | solution.py:630

commit v7 on v6

--- a/solution.py
+++ b/solution.py
@@ -508,7 +508,7 @@
             copy(2, ans_out.at[target], ans_in.at[me], target).start()
 
     total = jnp.zeros((1, LANES), f32)
-    turns = [*range(1, groups), 0]
+    turns = sorted(range(groups), key=lambda turn: -min(turn, groups - turn))
     begin(turns[0], 0)
     for n, turn in enumerate(turns):
         if n + 1 < groups:

time: 35 us -> 35 us (level)
  no operation moved by 1% of the time
where the time goes in v7:
time: 35 us; the launch traced here: 34.9 us
  Pallas kernels  34.2 us (98%)
  between operations  0.64 us (2%)
    pallas_call x1, Pallas kernels, shards(): pl.pallas_call(functools.partial(kernel, sizes), out_shape=(jax.ShapeDtyp...  33.5 us
    pallas_call x1, Pallas kernels, shards(): pl.pallas_call(functools.partial(finish, (float(amps_local * devices), fl...  0.71 us

profile of v7, /device:TPU:1, one launch (start us, length us, event | category | flops | bytes accessed | tf_op | source)
XLA Modules:
  0.0 34.9 jit_solution(8422749280678337461)
XLA Ops:
  0.6 33.5 %circuit.1 = (f32[64,128]{1,0:T(8,128)S(1)}, f32[1,128]{1,0:T(1,128)S(1)}, f32[1,128]{1,0:T(1,128)S(1)}) custom-call(f32[3,22]{1,0:T(4,128)} %bitcast.15, s32[1,10]{1,0:T(1,128)} %bitcast.16, f32[512,128]{1,0:T(8,128)} %bitcast.12, s32[64,128]{1,0:T(8,128)} %bitcast.13, s32[64,128]{1,0:T(8,128)} %bitcast.14), custom_call_target="tpu_custom_call" | custom-call | tf_op jit(solution)/shard_map/circuit/pallas_call | solution.py:579
  34.2 0.7 %finish.1 = (f32[64,128]{1,0:T(8,128)}, f32[1,8]{1,0:T(1,128)}, f32[1,1]{1,0:T(1,128)}) custom-call(f32[64,128]{1,0:T(8,128)S(1)} %get-tuple-element.9.values, f32[1,128]{1,0:T(1,128)S(1)} %get-tuple-element.10.hist, f32[1,128]{1,0:T(1,128)S(1)} %get-tuple-element.11.totals), custom_call_target="tpu_custom_call" | custom-call | tf_op jit(solution)/shard_map/finish/pallas_call | solution.py:630

commit v8 on v6

--- a/solution.py
+++ b/solution.py
@@ -178,15 +178,6 @@
     return both[:LANES] + both[LANES:]
 
 
-def lookup(table, upper, lower):
-    both = rows_dot(table, upper)
-    found = [
-        pick_lane(both[:, r * LANES : (r + 1) * LANES], lower[r : r + 1])
-        for r in range(upper.shape[0])
-    ]
-    return jnp.concatenate(found, axis=0)
-
-
 def lookup_lanes(plain, upper, lower):
     bits = plain.shape[0].bit_length() - 1
     high = [((upper >> bit) & 1) == 1 for bit in range(bits)]
@@ -199,16 +190,6 @@
         return jnp.where(high[bit], pick(first + (1 << bit), bit - 1), zero)
 
     return pick(0, bits - 1)
-
-
-def lookup_both(table, plain, upper, lower, lanes):
-    dots = upper.shape[0] - lanes
-    found = [lookup(table, upper[:dots], lower[:dots])]
-    for first in range(dots, dots + lanes, SUBLANES):
-        part = slice(first, first + SUBLANES)
-        value = lookup_lanes(plain, upper[part], lower[part])
-        found.append(jnp.where(upper[part] >= 0, value, 0.0))
-    return jnp.concatenate(found, axis=0)
 
 
 def routes(me):
@@ -528,11 +509,26 @@
     all_of(2, ans_in).wait_recv()
     plain_ref[0:codes] = join(ans_in[...])
     table_ref[:, 0:codes] = split_table(plain_ref[0:codes])
-    for first in range(0, samp_rows, 32):
-        window = slice(first, first + 32)
-        probs_ref[window] = lookup_both(
-            table_ref[:, 0:codes], plain_ref.at[0:codes], code_ref[window], rank_ref[window], 8
-        )
+    def fetch(block, slot):
+        window = slice(block * 32, (block + 1) * 32)
+        upper, lower = code_ref[window], rank_ref[window]
+        both_ref[slot] = rows_dot(table_ref[:, 0:codes], upper[:dots])
+        side_ref[slot] = lookup_lanes(plain_ref.at[0:codes], upper[dots:], lower[dots:])
+
+    def settle(block, slot):
+        lower = rank_ref[block * 32 : (block + 1) * 32]
+        found = [
+            pick_lane(both_ref[slot, :, r * LANES : (r + 1) * LANES], lower[r : r + 1])
+            for r in range(dots)
+        ]
+        probs_ref[block * 32 : (block + 1) * 32] = jnp.concatenate([*found, side_ref[slot]], axis=0)
+
+    blocks = samp_rows // 32
+    fetch(0, 0)
+    for block in range(blocks):
+        if block + 1 < blocks:
+            fetch(block + 1, (block + 1) % 2)
+        settle(block, block % 2)
     all_of(4, his_in).wait_recv()
     hist_ref[...] = jnp.sum(his_in[...], axis=0)
     all_of(3, tot_in).wait_recv()

time: 35 us -> 35 us (level)
  no operation moved by 1% of the time
where the time goes in v8:
time: 35 us; the launch traced here: 34.9 us
  Pallas kernels  34.2 us (98%)
  between operations  0.64 us (2%)
    pallas_call x1, Pallas kernels, shards(): pl.pallas_call(functools.partial(kernel, sizes), out_shape=(jax.ShapeDtyp...  33.5 us
    pallas_call x1, Pallas kernels, shards(): pl.pallas_call(functools.partial(finish, (float(amps_local * devices), fl...  0.71 us

profile of v8, /device:TPU:1, one launch (start us, length us, event | category | flops | bytes accessed | tf_op | source)
XLA Modules:
  0.0 34.9 jit_solution(6183549724407263046)
XLA Ops:
  0.6 33.5 %circuit.1 = (f32[64,128]{1,0:T(8,128)S(1)}, f32[1,128]{1,0:T(1,128)S(1)}, f32[1,128]{1,0:T(1,128)S(1)}) custom-call(f32[3,22]{1,0:T(4,128)} %bitcast.15, s32[1,10]{1,0:T(1,128)} %bitcast.16, f32[512,128]{1,0:T(8,128)} %bitcast.12, s32[64,128]{1,0:T(8,128)} %bitcast.13, s32[64,128]{1,0:T(8,128)} %bitcast.14), custom_call_target="tpu_custom_call" | custom-call | tf_op jit(solution)/shard_map/circuit/pallas_call | solution.py:575
  34.2 0.7 %finish.1 = (f32[64,128]{1,0:T(8,128)}, f32[1,8]{1,0:T(1,128)}, f32[1,1]{1,0:T(1,128)}) custom-call(f32[64,128]{1,0:T(8,128)S(1)} %get-tuple-element.9.values, f32[1,128]{1,0:T(1,128)S(1)} %get-tuple-element.10.hist, f32[1,128]{1,0:T(1,128)S(1)} %get-tuple-element.11.totals), custom_call_target="tpu_custom_call" | custom-call | tf_op jit(solution)/shard_map/finish/pallas_call | solution.py:626
